TPU v7x, 32 devices: a whole 2x2x4 slice. The times are simulated.
32 devices in a mesh: img: 4 (over y, core), proj: 8 (over z, x).
Axes of the slice: x: 2, y: 2, z: 4, core: 2. Of those that a mesh axis runs over, the one named last changes fastest.
Arguments:
- images: bfloat16 [512, 4096], P('img'), may hold values from -48 to 48
- projections: bfloat16 [2560, 4096], P('proj'), may hold values from -6 to 6
- noise_weight: float32 [4096], replicated, may hold values from 0.02 to 0.08
- defocus: float32 [512], P('img'), may hold values from 2 to 8
- orient_count: int32 [512], P('img'), may hold values from 160 to 2560, as said below
- term_limit: int32 [512], P('img'), may hold values from 2048 to 4096
- block_plan: int32 [16], replicated, may hold values from 0 to 15, each once
Outputs:
- reconstruction: bfloat16 [2560, 4096], P('proj', 'img')
- evidence_next: float32 [512], P('img')
Inputs may be any that keep to these rules, and one draw needn't show every extreme that they name: Orientations 0 to orient_count[i] - 1 are the significant ones of image i; some image has all 2560.
All inputs are finite; a program needn't handle non-finite values.
Results may differ from a plain program's by a relative error of at most 0.018.
Values may be sent and summed in bfloat16 or wider, within the bound.
A program may use at most 64 MiB of HBM per device.

v0:
```python
import math
import jax
import jax.numpy as jnp
from jax import lax
from jax.sharding import PartitionSpec as P

F = 4096
BLOCK = 32


def contrast_table(defocus, width):
    frequency = (jnp.arange(width, dtype=jnp.float32) + 1.0) / width
    return jnp.sin(2.0 * math.pi * defocus[:, None] * frequency[None, :] + 0.1)


def image_terms(pixels, noise_weight, defocus, limits):
    width = pixels.shape[1]
    contrast = contrast_table(defocus, width)
    keep_mask = (jnp.arange(width, dtype=jnp.int32)[None, :] < limits[:, None]).astype(jnp.float32)
    values = pixels.astype(jnp.float32)
    weighted = (keep_mask * noise_weight[None, :] * contrast * values).astype(jnp.bfloat16)
    weighted_sq = (keep_mask * noise_weight[None, :] * contrast * contrast).astype(jnp.bfloat16)
    back_images = (keep_mask * contrast * values).astype(jnp.bfloat16)
    return (weighted, weighted_sq, back_images)


def slice_weight_sums(every_post, focus_all, limit_all, start, slice_width, img_count, img_rows):
    term_ids = jnp.arange(slice_width, dtype=jnp.int32) + start
    term_float = term_ids.astype(jnp.float32)
    frequency = (term_float + 1.0) / F
    contrast = jnp.sin(2.0 * math.pi * focus_all[:, None] * frequency[None, :] + 0.1)
    keep_mask = (term_float[None, :] < limit_all[:, None]).astype(jnp.float32)
    rebuilt = (keep_mask * contrast * contrast).astype(jnp.bfloat16)
    rebuilt = rebuilt.reshape(img_count, img_rows, slice_width)
    partial_value = jnp.einsum(
        "jbi,bif->bjf", every_post, rebuilt, preferred_element_type=jnp.float32
    )
    partial_value = lax.optimization_barrier(partial_value.astype(jnp.bfloat16)).astype(jnp.float32)
    return jnp.sum(partial_value, axis=0)


def shards(images, projections, noise_weight, defocus, orient_count, term_limit, block_plan):
    proj_rows = projections.shape[0]
    img_rows = images.shape[0]
    weighted, weighted_sq, back_images = image_terms(images, noise_weight, defocus, term_limit)
    proj_sq = (projections.astype(jnp.float32) * projections.astype(jnp.float32)).astype(
        jnp.bfloat16
    )
    contract = (((1,), (1,)), ((), ()))
    scores = lax.dot_general(projections, weighted, contract, preferred_element_type=jnp.float32)
    scores = scores - 0.5 * lax.dot_general(
        proj_sq, weighted_sq, contract, preferred_element_type=jnp.float32
    )
    orient_ids = lax.axis_index("proj") * proj_rows + jnp.arange(proj_rows, dtype=jnp.int32)
    significant = orient_ids[:, None] < orient_count[None, :]
    local_peak = jnp.max(jnp.where(significant, scores, -1e30), axis=0)
    row_peak = lax.pmax(local_peak, "proj")
    safe = jnp.where(significant, scores, row_peak[None, :])
    local_mass = jnp.sum(jnp.where(significant, jnp.exp(safe - row_peak[None, :]), 0.0), axis=0)
    row_mass = lax.psum(local_mass, "proj")
    log_evidence = row_peak + jnp.log(row_mass)
    posterior = jnp.where(significant, jnp.exp(scores - log_evidence[None, :]), 0.0).astype(
        jnp.bfloat16
    )
    img_count = lax.axis_size("img")
    slice_width = F // img_count
    slice_start = lax.axis_index("img") * slice_width
    limit_float = term_limit.astype(jnp.float32)
    moved_images = lax.all_to_all(back_images, "img", split_axis=1, concat_axis=0, tiled=True)
    every_post = lax.all_gather(posterior, "img", axis=1, tiled=True)
    focus_all, limit_all = (
        lax.all_gather(defocus, "img", axis=0, tiled=True),
        lax.all_gather(limit_float, "img", axis=0, tiled=True),
    )
    every_post = every_post.reshape(proj_rows, img_count, img_rows)
    moved_images = moved_images.reshape(img_count, img_rows, slice_width)
    part_images = jnp.einsum(
        "jbi,bif->bjf", every_post, moved_images, preferred_element_type=jnp.float32
    )
    part_images = lax.optimization_barrier(part_images.astype(jnp.bfloat16)).astype(jnp.float32)
    sum_images = jnp.sum(part_images, axis=0)
    sum_weights = slice_weight_sums(
        every_post, focus_all, limit_all, slice_start, slice_width, img_count, img_rows
    )
    reconstruction = (sum_images / (sum_weights + 1.0)).astype(jnp.bfloat16)
    every_evidence = lax.all_gather(log_evidence, "img", axis=0, tiled=True)
    blocks = every_evidence.reshape(-1, BLOCK)
    local_blocks = img_rows // BLOCK
    slot_ids = lax.axis_index("img") * local_blocks + jnp.arange(local_blocks, dtype=jnp.int32)
    selector = (block_plan[None, :] == slot_ids[:, None]).astype(jnp.float32)
    own_blocks = jnp.dot(selector, blocks, precision=lax.Precision.HIGHEST)
    return (reconstruction, own_blocks.reshape(img_rows))


def solution(mesh):
    placed = (P("img", None), P("proj", None), P(), P("img"), P("img"), P("img"), P())
    return jax.shard_map(
        shards, mesh=mesh, in_specs=placed, out_specs=(P("proj", "img"), P("img")), check_vma=False
    )
```

profile of v0, /device:TPU:0, one launch (start us, length us, event | category | flops | bytes accessed | tf_op | source)
XLA Modules:
  0.0 115.0 jit_solution(12315028204032979167)
XLA Ops:
  0.6 0.0 copy-start.3
  0.7 0.7 broadcast_multiply_fusion.1
  1.3 1.6 %copy.15 = bf16[128,4096]{0,1:T(8,128)(2,1)S(1)} copy(bf16[128,4096]{1,0:T(8,128)(2,1)} %param.7) | data formatting | bytes 2097152 | tf_op args[0]
  2.9 8.5 %fusion.2 = bf16[128,4096]{0,1:T(8,128)(2,1)S(1)} fusion(bf16[128,4096]{0,1:T(8,128)(2,1)S(1)} %copy.15, f32[4096]{0:T(1024)S(1)} %add_multiply_fusion, f32[128]{0:T(128)S(1)} %broadcast_multiply_fusion.1, s32[128]{0:T(128)S(1)} %copy-done.3), kind=kLoop, calls=%fused_computation.8 | loop fusion | flops 3670016 | bytes 2114560 | tf_op jit(solution)/shard_map/convert_element_type | solution.py:23
  11.4 0.0 copy-start.5
  11.4 1.3 %copy.16 = bf16[128,4,1024]{2,0,1:T(8,128)(2,1)} copy(bf16[128,4,1024]{0,2,1:T(8,128)(2,1)S(1)} %bitcast.26) | data formatting | bytes 2097152 | tf_op jit(solution)/shard_map/all_to_all | solution.py:69
  12.7 4.3 %all-to-all-start = ((bf16[128,4,1024]{2,0,1:T(8,128)(2,1)}), bf16[128,4,1024]{2,0,1:T(8,128)(2,1)S(1)}, u32[]{:S(2)}, u32[]{:S(2)}) async-start(bf16[128,4,1024]{2,0,1:T(8,128)(2,1)} %copy.16), calls=%async_computation | async-start | bytes 2097152 | tf_op jit(solution)/shard_map/all_to_all | solution.py:69
  17.0 0.0 copy-start.1
  17.0 0.0 copy-start.4
  17.1 12.5 %convolution_bitcast_fusion = f32[320,128]{1,0:T(8,128)S(1)} fusion(bf16[320,4096]{1,0:T(8,128)(2,1)} %param.8, bf16[128,4096]{0,1:T(8,128)(2,1)S(1)} %copy.15, f32[4096]{0:T(1024)S(1)} %add_multiply_fusion, f32[128]{0:T(128)S(1)} %broadcast_multiply_fusion.1, f32[4096]{0:T(1024)S(1)} %copy-done.5, s32[128]{0:T(128)S(1)} %copy-done.3), kind=kOutput, calls=%fused_computation.19 | convolution fusion | flops 339738624 | bytes 3867648 | tf_op jit(solution)/shard_map/dot_general | solution.py:50
  29.6 0.0 copy-start.6
  29.6 0.0 copy-start.2
  29.6 8.2 %fusion.32 = (f32[128]{0:T(128)S(1)}, f32[320,128]{1,0:T(8,128)S(1)}) fusion(s32[128]{0:T(128)S(1)} %copy-done.1, s32[320]{0:T(512)S(1)} %iota_add_fusion, f32[320,128]{1,0:T(8,128)S(1)} %convolution_bitcast_fusion, f32[4096]{0:T(1024)S(1)} %add_multiply_fusion, f32[128]{0:T(128)S(1)} %broadcast_multiply_fusion.1, f32[4096]{0:T(1024)S(1)} %copy-done.5, ...), kind=kOutput, calls=%fused_computation.47 | convolution fusion | flops 343351168 | bytes 2985216 | tf_op jit(solution)/shard_map/dot_general | solution.py:51
  37.7 22.6 %pmax.7 = f32[128]{0:T(128)S(1)} all-reduce(f32[128]{0:T(128)S(1)} %get-tuple-element.2), channel_id=1, replica_groups=mesh['img'=4,'proj'=8] {'proj'}, use_global_device_ids=true, to_apply=%region_1.2 | all-reduce | flops 128 | bytes 1024 | tf_op jit(solution)/shard_map/pmax | solution.py:57
  60.3 0.1 fusion.35
  60.5 17.1 %psum.7 = f32[128]{0:T(128)S(1)} all-reduce(f32[128]{0:T(128)S(1)} %fusion.35), channel_id=1, replica_groups=mesh['img'=4,'proj'=8] {'proj'}, use_global_device_ids=true, to_apply=%region_3.4 | all-reduce | flops 128 | bytes 1024 | tf_op jit(solution)/shard_map/psum | solution.py:60
  77.6 0.1 fusion.36
  77.7 5.1 %all-gather.2 = f32[4,1,128]{2,1,0:T(1,128)S(1)} all-gather(f32[1,1,128]{2,1,0:T(1,128)S(1)} %bitcast.27), channel_id=1, replica_groups=mesh['img'=4,'proj'=8] {'img'}, dimensions={0}, use_global_device_ids=true | all-gather | bytes 2560 | tf_op jit(solution)/shard_map/all_gather | solution.py:86
  82.8 0.5 broadcast.84
  83.3 0.7 reduce.3
  84.0 0.1 reshape.73
  84.0 0.2 fusion.37
  84.2 0.6 reshape.74
  84.8 5.3 %all-gather = f32[4,1,128]{2,1,0:T(1,128)S(1)} all-gather(f32[1,1,128]{2,1,0:T(1,128)S(1)} %convert_bitcast_fusion), channel_id=1, replica_groups=mesh['img'=4,'proj'=8] {'img'}, dimensions={0}, use_global_device_ids=true | all-gather | bytes 2560 | tf_op jit(solution)/shard_map/all_gather | solution.py:73
  90.1 5.0 %all-gather.1 = f32[4,1,128]{2,1,0:T(1,128)S(1)} all-gather(f32[1,1,128]{2,1,0:T(1,128)S(1)} %bitcast.30), channel_id=1, replica_groups=mesh['img'=4,'proj'=8] {'img'}, dimensions={0}, use_global_device_ids=true | all-gather | bytes 2560 | tf_op jit(solution)/shard_map/all_gather | solution.py:72
  95.2 6.3 %all_gather.12 = bf16[320,512]{1,0:T(8,128)(2,1)S(1)} all-gather(bf16[320,128]{1,0:T(8,128)(2,1)S(1)} %fusion.36), channel_id=1, replica_groups=mesh['img'=4,'proj'=8] {'img'}, dimensions={1}, use_global_device_ids=true | all-gather | bytes 409600 | tf_op jit(solution)/shard_map/all_gather | solution.py:70
  101.5 9.4 %convolution_convert_fusion = bf16[4,320,1024]{2,1,0:T(8,128)(2,1)} fusion(f32[1024]{0:T(1024)S(1)} %add_multiply_fusion.1, f32[4,128]{1,0:T(4,128)S(1)} %bitcast.29, f32[4,128]{1,0:T(4,128)S(1)} %bitcast.28, f32[1024]{0:T(1024)S(1)} %add_convert_fusion, bf16[320,512]{1,0:T(8,128)(2,1)S(1)} %all_gather.12), kind=kOutput, calls=%fused_computation.14 | convolution fusion | flops 340000768 | bytes 2961408 | tf_op jit(solution)/shard_map/jbi,bif->bjf/dot_general | solution.py:35
  110.9 0.0 all-to-all-done
  110.9 0.8 convolution_convert_fusion.1
  111.8 0.9 copy-done
  112.7 1.2 %convert_reduce_fusion = (f32[320,1024]{1,0:T(8,128)S(1)}, f32[320,1024]{1,0:T(8,128)S(1)}) fusion(bf16[4,320,1024]{2,1,0:T(8,128)(2,1)S(1)} %copy-done, bf16[4,320,1024]{2,1,0:T(8,128)(2,1)S(1)} %convolution_convert_fusion.1), kind=kLoop, calls=%fused_computation | loop fusion | flops 4587520 | bytes 7864320 | tf_op jit(solution)/shard_map/reduce_sum | solution.py:39
  113.9 1.1 divide_convert_fusion
  (15 shorter events, 0.1 us)
Async XLA Ops:
  0.6 2.3 %copy-start.3 = (s32[128]{0:T(128)S(1)}, s32[128]{0:T(128)}, u32[]{:S(2)}) copy-start(s32[128]{0:T(128)} %param.12) | copy-start | bytes 1540
  11.4 5.6 %copy-start.5 = (f32[4096]{0:T(1024)S(1)}, f32[4096]{0:T(1024)}, u32[]{:S(2)}) copy-start(f32[4096]{0:T(1024)} %param.9) | copy-start | bytes 49156
  12.7 98.2 %all-to-all-start = ((bf16[128,4,1024]{2,0,1:T(8,128)(2,1)}), bf16[128,4,1024]{2,0,1:T(8,128)(2,1)S(1)}, u32[]{:S(2)}, u32[]{:S(2)}) async-start(bf16[128,4,1024]{2,0,1:T(8,128)(2,1)} %copy.16), calls=%async_computation | async-start | bytes 2097152 | tf_op jit(solution)/shard_map/all_to_all | solution.py:69
  17.0 12.5 %copy-start.1 = (s32[128]{0:T(128)S(1)}, s32[128]{0:T(128)}, u32[]{:S(2)}) copy-start(s32[128]{0:T(128)} %param.11) | copy-start | bytes 1540
  17.0 12.5 %copy-start.4 = (bf16[320,4096]{1,0:T(8,128)(2,1)S(1)}, bf16[320,4096]{1,0:T(8,128)(2,1)}, u32[]{:S(2)}) copy-start(bf16[320,4096]{1,0:T(8,128)(2,1)} %param.8) | copy-start | bytes 7864324
  29.6 54.5 %copy-start.6 = (s32[16]{0:T(128)S(1)}, s32[16]{0:T(128)}, u32[]{:S(2)}) copy-start(s32[16]{0:T(128)} %param.13) | copy-start | bytes 196
  29.6 60.6 %copy-start.2 = (f32[128]{0:T(128)S(1)}, f32[128]{0:T(128)}, u32[]{:S(2)}) copy-start(f32[128]{0:T(128)} %param.10) | copy-start | bytes 1540
  110.9 1.7 %copy-start = (bf16[4,320,1024]{2,1,0:T(8,128)(2,1)S(1)}, bf16[4,320,1024]{2,1,0:T(8,128)(2,1)}, u32[]{:S(2)}) copy-start(bf16[4,320,1024]{2,1,0:T(8,128)(2,1)} %convolution_convert_fusion) | copy-start | bytes 7864324
where the time goes:
time: 115 us
  blocking collectives  61.5 us (53%)
  matrix products  31 us (27%)
  other arithmetic  12.4 us (11%)
  local copies, waits for them, and re-layouts  5.05 us (4%)
  starting transfers between devices  4.26 us (4%)
    pmax x1, blocking collectives, shards(): row_peak = lax.pmax(local_peak, 'proj')  22.6 us
    psum x1, blocking collectives, shards(): row_mass = lax.psum(local_mass, 'proj')  17.1 us
    dot_general x1, matrix products, shards(): lax.dot_general(projections, weighted, contract, preferred_element_type=j...  12.5 us
    dot_general x1, matrix products, slice_weight_sums(): jnp.einsum('jbi,bif->bjf', every_post, rebuilt, preferred_element_type=jn...  9.38 us
    convert_element_type x1, other arithmetic, image_terms(): back_images = (keep_mask * contrast * values).astype(jnp.bfloat16)  8.45 us
    dot_general x1, matrix products, shards(): lax.dot_general(proj_sq, weighted_sq, contract, preferred_element_type=jn...  8.17 us
    all_gather x1, blocking collectives, shards(): every_post = lax.all_gather(posterior, 'img', axis=1, tiled=True)  6.34 us
    all_gather x1, blocking collectives, shards(): lax.all_gather(limit_float, 'img', axis=0, tiled=True)  5.29 us
  transfers between devices with their start and end apart: 1, of which 0 were waited for; matrix products, arithmetic and copies ran while one was open for 28% of the time, Pallas kernels for 0%

commit v1 on v0

--- a/solution.py
+++ b/solution.py
@@ -67,7 +67,24 @@
     slice_start = lax.axis_index("img") * slice_width
     limit_float = term_limit.astype(jnp.float32)
     moved_images = lax.all_to_all(back_images, "img", split_axis=1, concat_axis=0, tiled=True)
-    every_post = lax.all_gather(posterior, "img", axis=1, tiled=True)
+    n_now = jax.lax.axis_size("img")
+    carry_out = jax.lax.axis_index("img")
+    finding, u_next, e_next = (n_now, carry_out, posterior.shape[1])
+    fresh = jnp.zeros(
+        [no * finding if s == 1 else no for s, no in enumerate(posterior.shape)], posterior.dtype
+    )
+    x_now = val2 = posterior
+    every_post = lax.dynamic_update_slice_in_dim(fresh, posterior, u_next * e_next, axis=1)
+    for tick in range(1, finding // 2 + 1):
+        x_now = jax.lax.ppermute(x_now, "img", [(s, (s + 1) % finding) for s in range(finding)])
+        every_post = lax.dynamic_update_slice_in_dim(
+            every_post, x_now, (u_next - tick) % finding * e_next, axis=1
+        )
+        if 2 * tick < finding:
+            val2 = jax.lax.ppermute(val2, "img", [(s, (s - 1) % finding) for s in range(finding)])
+            every_post = lax.dynamic_update_slice_in_dim(
+                every_post, val2, (u_next + tick) % finding * e_next, axis=1
+            )
     focus_all, limit_all = (
         lax.all_gather(defocus, "img", axis=0, tiled=True),
         lax.all_gather(limit_float, "img", axis=0, tiled=True),

time: 115 us -> 124 us (1.078)
  blocking collectives: 61.5 us -> 65.6 us
  waiting for transfers between devices: 0.01 us -> 3.46 us
  starting transfers between devices: 4.26 us -> 5.65 us
    all_gather x1, blocking collectives: 5.05 us -> 15.3 us  [shards(): lax.all_gather(defocus, 'img', axis=0, tiled=True)]
    all_gather x1 -> x0, blocking collectives: 6.34 us -> none  [shards(): every_post = lax.all_gather(posterior, 'img', axis=1, tiled=True)]
    ppermute x0 -> x3, waiting for transfers between devices: none -> 3.46 us  [the longest x2 3.46 us: shards(): jax.lax.ppermute(x_now, 'img', [(s, (s + 1) % finding) for s in range(fin...]
    ppermute x0 -> x3, starting transfers between devices: none -> 2.13 us  [the longest x1 1.73 us: shards(): jax.lax.ppermute(val2, 'img', [(s, (s - 1) % finding) for s in range(find...]
  transfers between devices with their start and end apart: 1 -> 4, of which waited for: 0 -> 1; matrix products, arithmetic and copies ran while one was open for 28% -> 17% of each run, Pallas kernels for 0% -> 0%
where the time goes in v1:
time: 124 us
  blocking collectives  65.6 us (53%)
  matrix products  31 us (25%)
  other arithmetic  12.3 us (10%)
  starting transfers between devices  5.65 us (5%)
  local copies, waits for them, and re-layouts  5.14 us (4%)
  waiting for transfers between devices  3.46 us (3%)
    pmax x1, blocking collectives, shards(): row_peak = lax.pmax(local_peak, 'proj')  23.1 us
    psum x1, blocking collectives, shards(): row_mass = lax.psum(local_mass, 'proj')  17.1 us
    all_gather x1, blocking collectives, shards(): lax.all_gather(defocus, 'img', axis=0, tiled=True)  15.3 us
    dot_general x1, matrix products, shards(): lax.dot_general(projections, weighted, contract, preferred_element_type=j...  12.5 us
    dot_general x1, matrix products, slice_weight_sums(): jnp.einsum('jbi,bif->bjf', every_post, rebuilt, preferred_element_type=jn...  9.4 us
    convert_element_type x1, other arithmetic, image_terms(): back_images = (keep_mask * contrast * values).astype(jnp.bfloat16)  8.43 us
    dot_general x1, matrix products, shards(): lax.dot_general(proj_sq, weighted_sq, contract, preferred_element_type=jn...  8.17 us
    all_gather x1, blocking collectives, shards(): every_evidence = lax.all_gather(log_evidence, 'img', axis=0, tiled=True)  5.05 us
  transfers between devices with their start and end apart: 4, of which 1 were waited for; matrix products, arithmetic and copies ran while one was open for 17% of the time, Pallas kernels for 0%

profile of v1, /device:TPU:0, one launch (start us, length us, event | category | flops | bytes accessed | tf_op | source)
XLA Modules:
  0.0 124.1 jit_solution(16071978938008712671)
XLA Ops:
  0.7 0.7 broadcast_multiply_fusion.1
  1.3 1.6 %copy.13 = bf16[128,4096]{0,1:T(8,128)(2,1)S(1)} copy(bf16[128,4096]{1,0:T(8,128)(2,1)} %param.7) | data formatting | bytes 2097152 | tf_op args[0]
  3.0 0.0 copy-start.1
  3.0 0.0 copy-start.4
  3.0 12.5 %convolution_bitcast_fusion = f32[320,128]{1,0:T(8,128)S(1)} fusion(bf16[320,4096]{1,0:T(8,128)(2,1)} %param.8, bf16[128,4096]{0,1:T(8,128)(2,1)S(1)} %copy.13, f32[4096]{0:T(1024)S(1)} %add_multiply_fusion, f32[128]{0:T(128)S(1)} %broadcast_multiply_fusion.1, f32[4096]{0:T(1024)S(1)} %copy-done.5, s32[128]{0:T(128)S(1)} %copy-done.3), kind=kOutput, calls=%fused_computation.19 | convolution fusion | flops 339738624 | bytes 3867648 | tf_op jit(solution)/shard_map/dot_general | solution.py:50
  15.5 8.2 %fusion.32 = (f32[128]{0:T(128)S(1)}, f32[320,128]{1,0:T(8,128)S(1)}) fusion(s32[128]{0:T(128)S(1)} %copy-done.1, s32[320]{0:T(512)S(1)} %iota_add_fusion, f32[320,128]{1,0:T(8,128)S(1)} %convolution_bitcast_fusion, f32[4096]{0:T(1024)S(1)} %add_multiply_fusion, f32[128]{0:T(128)S(1)} %broadcast_multiply_fusion.1, f32[4096]{0:T(1024)S(1)} %copy-done.5, ...), kind=kOutput, calls=%fused_computation.47 | convolution fusion | flops 343351168 | bytes 2985216 | tf_op jit(solution)/shard_map/dot_general | solution.py:51
  23.7 23.1 %pmax.7 = f32[128]{0:T(128)S(1)} all-reduce(f32[128]{0:T(128)S(1)} %get-tuple-element.4), channel_id=1, replica_groups=mesh['img'=4,'proj'=8] {'proj'}, use_global_device_ids=true, to_apply=%region_1.2 | all-reduce | flops 128 | bytes 1024 | tf_op jit(solution)/shard_map/pmax | solution.py:57
  46.8 0.1 fusion.35
  46.9 17.1 %psum.7 = f32[128]{0:T(128)S(1)} all-reduce(f32[128]{0:T(128)S(1)} %fusion.35), channel_id=1, replica_groups=mesh['img'=4,'proj'=8] {'proj'}, use_global_device_ids=true, to_apply=%region_3.4 | all-reduce | flops 128 | bytes 1024 | tf_op jit(solution)/shard_map/psum | solution.py:60
  64.1 0.1 constant_dynamic-update-slice_fusion.3
  64.2 0.1 collective-permute-start
  64.3 1.7 %collective-permute-start.1 = (bf16[320,128]{1,0:T(8,128)(2,1)S(1)}, bf16[320,128]{1,0:T(8,128)(2,1)S(1)}, u32[]{:S(2)}, u32[]{:S(2)}) collective-permute-start(bf16[320,128]{1,0:T(8,128)(2,1)S(1)} %get-tuple-element.3), channel_id=1, source_target_pairs={{0,24},{8,0},{16,8},{24,16},{1,25},{9,1},{17,9},{25,17},{2,26},{10... | collective-permute-start | bytes 245768 | tf_op jit(solution)/shard_map/ppermute | solution.py:84
  66.0 8.4 %fusion.2 = bf16[128,4096]{0,1:T(8,128)(2,1)S(1)} fusion(bf16[128,4096]{0,1:T(8,128)(2,1)S(1)} %copy.13, f32[4096]{0:T(1024)S(1)} %add_multiply_fusion, f32[128]{0:T(128)S(1)} %broadcast_multiply_fusion.1, s32[128]{0:T(128)S(1)} %copy-done.3), kind=kLoop, calls=%fused_computation.8 | loop fusion | flops 3670016 | bytes 2114560 | tf_op jit(solution)/shard_map/convert_element_type | solution.py:23
  74.5 0.0 copy-start.2
  74.5 0.0 copy-start.6
  74.5 1.3 %copy.14 = bf16[128,4,1024]{2,0,1:T(8,128)(2,1)} copy(bf16[128,4,1024]{0,2,1:T(8,128)(2,1)S(1)} %bitcast.26) | data formatting | bytes 2097152 | tf_op jit(solution)/shard_map/all_to_all | solution.py:69
  75.8 3.5 %all-to-all-start = ((bf16[128,4,1024]{2,0,1:T(8,128)(2,1)}), bf16[128,4,1024]{2,0,1:T(8,128)(2,1)S(1)}, u32[]{:S(2)}, u32[]{:S(2)}) async-start(bf16[128,4,1024]{2,0,1:T(8,128)(2,1)} %copy.14), calls=%async_computation | async-start | bytes 2097152 | tf_op jit(solution)/shard_map/all_to_all | solution.py:69
  79.4 15.3 %all-gather.1 = f32[4,1,128]{2,1,0:T(1,128)S(1)} all-gather(f32[1,1,128]{2,1,0:T(1,128)S(1)} %bitcast.30), channel_id=1, replica_groups=mesh['img'=4,'proj'=8] {'img'}, dimensions={0}, use_global_device_ids=true | all-gather | bytes 2560 | tf_op jit(solution)/shard_map/all_gather | solution.py:89
  94.6 5.0 %all-gather.2 = f32[4,1,128]{2,1,0:T(1,128)S(1)} all-gather(f32[1,1,128]{2,1,0:T(1,128)S(1)} %bitcast.29), channel_id=1, replica_groups=mesh['img'=4,'proj'=8] {'img'}, dimensions={0}, use_global_device_ids=true | all-gather | bytes 2560 | tf_op jit(solution)/shard_map/all_gather | solution.py:103
  99.7 0.5 broadcast.87
  100.2 0.7 reduce.3
  100.9 0.1 reshape.73
  100.9 0.2 fusion.37
  101.1 0.6 reshape.74
  101.7 5.0 %all-gather = f32[4,1,128]{2,1,0:T(1,128)S(1)} all-gather(f32[1,1,128]{2,1,0:T(1,128)S(1)} %convert_bitcast_fusion), channel_id=1, replica_groups=mesh['img'=4,'proj'=8] {'img'}, dimensions={0}, use_global_device_ids=true | all-gather | bytes 2560 | tf_op jit(solution)/shard_map/all_gather | solution.py:90
  106.8 0.3 collective-permute-start.2
  107.2 3.5 %collective-permute-done.2 = bf16[320,128]{1,0:T(8,128)(2,1)S(1)} collective-permute-done((bf16[320,128]{1,0:T(8,128)(2,1)S(1)}, bf16[320,128]{1,0:T(8,128)(2,1)S(1)}, u32[]{:S(2)}, u32[]{:S(2)}) %collective-permute-start.2) | collective-permute-done | bytes 81952 | tf_op jit(solution)/shard_map/ppermute | solution.py:79
  110.7 9.4 %convolution_convert_fusion = bf16[4,320,1024]{2,1,0:T(8,128)(2,1)} fusion(f32[1024]{0:T(1024)S(1)} %add_multiply_fusion.1, f32[4,128]{1,0:T(4,128)S(1)} %bitcast.28, f32[4,128]{1,0:T(4,128)S(1)} %bitcast.27, f32[1024]{0:T(1024)S(1)} %add_convert_fusion, bf16[320,512]{1,0:T(8,128)(2,1)S(1)} %constant_dynamic-update-slice_fusion), kind=kOutput, calls=%fused_computation.14 | convolution fusion | flops 340000768 | bytes 2961408 | tf_op jit(solution)/shard_map/jbi,bif->bjf/dot_general | solution.py:35
  120.1 0.8 convolution_convert_fusion.1
  120.9 0.9 copy-done
  121.8 1.2 convert_reduce_fusion
  123.1 1.1 divide_convert_fusion
  (24 shorter events, 0.2 us)
Async XLA Ops:
  0.6 2.3 %copy-start.3 = (s32[128]{0:T(128)S(1)}, s32[128]{0:T(128)}, u32[]{:S(2)}) copy-start(s32[128]{0:T(128)} %param.12) | copy-start | bytes 1540
  0.6 2.3 %copy-start.5 = (f32[4096]{0:T(1024)S(1)}, f32[4096]{0:T(1024)}, u32[]{:S(2)}) copy-start(f32[4096]{0:T(1024)} %param.9) | copy-start | bytes 49156
  3.0 12.5 %copy-start.1 = (s32[128]{0:T(128)S(1)}, s32[128]{0:T(128)}, u32[]{:S(2)}) copy-start(s32[128]{0:T(128)} %param.11) | copy-start | bytes 1540
  3.0 12.5 %copy-start.4 = (bf16[320,4096]{1,0:T(8,128)(2,1)S(1)}, bf16[320,4096]{1,0:T(8,128)(2,1)}, u32[]{:S(2)}) copy-start(bf16[320,4096]{1,0:T(8,128)(2,1)} %param.8) | copy-start | bytes 7864324
  64.2 42.6 %collective-permute-start = (bf16[320,128]{1,0:T(8,128)(2,1)S(1)}, bf16[320,128]{1,0:T(8,128)(2,1)S(1)}, u32[]{:S(2)}, u32[]{:S(2)}) collective-permute-start(bf16[320,128]{1,0:T(8,128)(2,1)S(1)} %get-tuple-element.3), channel_id=1, source_target_pairs={{0,8},{8,16},{16,24},{24,0},{1,9},{9,17},{17,25},{25,1},{2,10},{10... | collective-permute-start | bytes 245768 | tf_op jit(solution)/shard_map/ppermute | solution.py:79
  64.3 42.9 %collective-permute-start.1 = (bf16[320,128]{1,0:T(8,128)(2,1)S(1)}, bf16[320,128]{1,0:T(8,128)(2,1)S(1)}, u32[]{:S(2)}, u32[]{:S(2)}) collective-permute-start(bf16[320,128]{1,0:T(8,128)(2,1)S(1)} %get-tuple-element.3), channel_id=1, source_target_pairs={{0,24},{8,0},{16,8},{24,16},{1,25},{9,1},{17,9},{25,17},{2,26},{10... | collective-permute-start | bytes 245768 | tf_op jit(solution)/shard_map/ppermute | solution.py:84
  74.5 4.9 %copy-start.2 = (f32[128]{0:T(128)S(1)}, f32[128]{0:T(128)}, u32[]{:S(2)}) copy-start(f32[128]{0:T(128)} %param.10) | copy-start | bytes 1540
  74.5 26.5 %copy-start.6 = (s32[16]{0:T(128)S(1)}, s32[16]{0:T(128)}, u32[]{:S(2)}) copy-start(s32[16]{0:T(128)} %param.13) | copy-start | bytes 196
  75.8 44.3 %all-to-all-start = ((bf16[128,4,1024]{2,0,1:T(8,128)(2,1)}), bf16[128,4,1024]{2,0,1:T(8,128)(2,1)S(1)}, u32[]{:S(2)}, u32[]{:S(2)}) async-start(bf16[128,4,1024]{2,0,1:T(8,128)(2,1)} %copy.14), calls=%async_computation | async-start | bytes 2097152 | tf_op jit(solution)/shard_map/all_to_all | solution.py:69
  106.8 3.9 %collective-permute-start.2 = (bf16[320,128]{1,0:T(8,128)(2,1)S(1)}, bf16[320,128]{1,0:T(8,128)(2,1)S(1)}, u32[]{:S(2)}, u32[]{:S(2)}) collective-permute-start(bf16[320,128]{1,0:T(8,128)(2,1)S(1)} %collective-permute-done), channel_id=1, source_target_pairs={{0,8},{8,16},{16,24},{24,0},{1,9},{9,17},{17,25},{25,1},{2,10},{10... | collective-permute-start | bytes 245768 | tf_op jit(solution)/shard_map/ppermute | solution.py:79
  120.1 1.7 %copy-start = (bf16[4,320,1024]{2,1,0:T(8,128)(2,1)S(1)}, bf16[4,320,1024]{2,1,0:T(8,128)(2,1)}, u32[]{:S(2)}) copy-start(bf16[4,320,1024]{2,1,0:T(8,128)(2,1)} %convolution_convert_fusion) | copy-start | bytes 7864324
